TPU v7x, 32 devices: a whole 2x2x4 slice. The times are simulated.
32 devices in a mesh: gz: 8 (over z, y), gy: 4 (over x, core).
Axes of the slice: x: 2, y: 2, z: 4, core: 2. Of those that a mesh axis runs over, the one named last changes fastest.
Arguments:
- orbitals: bfloat16 [96, 96, 96, 256], P('gz', 'gy'), may hold values from -6 to 6
- pair_list: int32 [64, 2], replicated, may hold values from 0 to 255
- box_anchor: int32 [256, 3], replicated, may hold values from 0 to 95
- pair_live: int32 [64], replicated, may hold values from 0 to 1, as said below
Outputs:
- gradient: float32 [96, 96, 96, 256], P('gz', 'gy')
Inputs may be any that keep to these rules, and one draw needn't show every extreme that they name: `pair_live`: in each owner's block of 2 slots the live slots come first; at least one slot of every block is live, some block has all 2 live, and some other block has exactly one live.
All inputs are finite; a program needn't handle non-finite values.
Results may differ from a plain program's by a relative error of at most 0.0035.
Values may be sent and summed in bfloat16 or wider, within the bound.
A program may use at most 192 MiB of HBM per device.

v0:
```python
import jax
import jax.numpy as jnp
from jax import lax
from jax.sharding import PartitionSpec as P

B = 64


def poisson_box(density):
    side = density.shape[-1]
    index = jnp.arange(1, side + 1).astype(jnp.float32)
    table = jnp.sqrt(2.0 / (side + 1.0)) * jnp.sin(
        jnp.pi * index[:, None] * index[None, :] / (side + 1.0)
    )
    eigen = 2.0 - 2.0 * jnp.cos(jnp.pi * index / (side + 1.0))
    denom = eigen[:, None, None] + eigen[None, :, None] + eigen[None, None, :]
    hp = lax.Precision.HIGHEST

    def apply_all(field):
        field = jnp.einsum("...abc,ai->...ibc", field, table, precision=hp)
        field = jnp.einsum("...ibc,bj->...ijc", field, table, precision=hp)
        return jnp.einsum("...ijc,ck->...ijk", field, table, precision=hp)

    return apply_all(apply_all(density) / denom)


def body(orbitals, pair_list, box_anchor, pair_live):
    depth, rows, across, norb = orbitals.shape
    n_gz = lax.axis_size("gz")
    n_gy = lax.axis_size("gy")
    owners = n_gz * n_gy
    pairs = pair_list.shape[0]
    per_dev = pairs // owners
    slots = 2 * per_dev
    side = B
    extent = depth * n_gz
    firsts = pair_list[:, 0]
    chosen = jnp.take(orbitals, pair_list.reshape(-1), axis=3)
    width = chosen.shape[2]
    outgoing = chosen.reshape(depth, rows, width, n_gz, n_gy, slots)
    flat_send = outgoing.reshape(depth, rows, width, owners, slots)
    incoming = lax.all_to_all(
        flat_send, ("gz", "gy"), split_axis=3, concat_axis=3, tiled=True
    ).reshape(depth, rows, width, n_gz, n_gy, slots)
    grids = jnp.transpose(incoming, (5, 3, 0, 4, 1, 2)).reshape(per_dev, 2, extent, extent, width)
    owner = lax.axis_index(("gz", "gy"))
    mine = lax.dynamic_slice_in_dim(pair_list, owner * per_dev, per_dev, 0)
    live = lax.dynamic_slice_in_dim(pair_live, owner * per_dev, per_dev, 0)
    anchors = box_anchor[mine[:, 0]]

    def cut_box(grid, anchor):
        grid = jnp.roll(grid, -anchor[0], axis=0)
        grid = jnp.roll(grid, -anchor[1], axis=1)
        grid = jnp.roll(grid, -anchor[2], axis=2)
        return grid[:side, :side, :side]

    def both_boxes(pair_grids, anchor):
        return jax.vmap(cut_box, in_axes=(0, None))(pair_grids, anchor)

    boxes = jax.vmap(both_boxes)(grids, anchors)
    left = boxes[:, 0].astype(jnp.float32)
    right = boxes[:, 1].astype(jnp.float32)
    potential = poisson_box(left * right)
    weight = live.astype(jnp.float32)[:, None, None, None]
    term = (potential * right * weight).astype(jnp.bfloat16)

    def place_box(box, anchor):
        pad_x = across - side
        grid = jnp.pad(box, ((0, extent - side), (0, extent - side), (0, pad_x)))
        grid = jnp.roll(grid, anchor[0], axis=0)
        grid = jnp.roll(grid, anchor[1], axis=1)
        grid = jnp.roll(grid, anchor[2], axis=2)
        return grid

    placed = jax.vmap(place_box)(term, anchors)
    back_send = jnp.transpose(
        placed.reshape(per_dev, n_gz, depth, n_gy, rows, width), (2, 4, 5, 1, 3, 0)
    )
    flat_back = back_send.reshape(depth, rows, width, owners, per_dev)
    back = lax.all_to_all(flat_back, ("gz", "gy"), split_axis=3, concat_axis=3, tiled=True)
    contrib = back.reshape(depth, rows, width, pairs)
    selector = (firsts[:, None] == jnp.arange(norb)[None, :]).astype(jnp.bfloat16)
    action = jnp.dot(contrib.reshape(-1, pairs), selector, preferred_element_type=jnp.float32)
    action_low = action.astype(jnp.bfloat16)
    flat = orbitals.reshape(-1, norb)
    partial_tiles = lax.dot_general(
        flat, action_low, (((0,), (0,)), ((), ())), preferred_element_type=jnp.float32
    )
    summed = lax.psum(partial_tiles, ("gz", "gy"))
    tiles = (summed / (float(B) ** 3 / 4.0)).astype(jnp.bfloat16)
    gradient = action - jnp.dot(flat, tiles, preferred_element_type=jnp.float32)
    return gradient.reshape(depth, rows, across, norb)


def solution(mesh):
    return jax.shard_map(
        body,
        mesh=mesh,
        in_specs=(P("gz", "gy", None, None), P(), P(), P()),
        out_specs=P("gz", "gy", None, None),
        check_vma=False,
    )
```

profile of v0, /device:TPU:0, one launch (start us, length us, event | category | flops | bytes accessed | tf_op | source)
XLA Modules:
  0.0 842.0 jit_solution(8082996493727971002)
XLA Ops:
  7.5 22.4 %copy.44 = bf16[12,24,96,256]{2,1,0,3:T(8,128)(2,1)} copy(bf16[12,24,96,256]{3,2,1,0:T(8,128)(2,1)} %param.4) | data formatting | bytes 28311552 | tf_op args[0]
  29.9 13.6 %gather_fusion = bf16[128,12,24,96]{3,2,1,0:T(8,128)(2,1)} fusion(bf16[12,24,96,256]{2,1,0,3:T(8,128)(2,1)} %copy.44, s32[1024]{0:T(1024)S(1)} %pad_clamp_fusion.1), kind=kCustom, calls=%fused_computation | custom fusion | bytes 14156288 | tf_op jit(solution)/shard_map/jit(_take)/gather | solution.py:38
  43.5 9.6 %copy.45 = bf16[12,24,96,128]{2,1,3,0:T(8,128)(2,1)} copy(bf16[12,24,96,128]{2,1,0,3:T(8,128)(2,1)} %bitcast.113) | data formatting | bytes 14155776 | tf_op jit(solution)/shard_map/jit(_take)/gather | solution.py:38
  53.2 8.6 %broadcast_select_fusion = bf16[12,24,96,32,4]{2,1,4,3,0:T(8,128)(2,1)} fusion(bf16[12,24,96,32,4]{2,1,4,3,0:T(8,128)(2,1)} %bitcast.112, pred[32,4]{1,0:T(8,128)(4,1)S(1)} %compare_and_fusion), kind=kLoop, calls=%fused_computation.24 | loop fusion | flops 3538944 | bytes 14155904 | tf_op jit(solution)/shard_map/jit(_take)/select_n | solution.py:38
  61.7 10.2 %copy.46 = bf16[12,24,96,32,4]{2,1,4,0,3:T(8,128)(2,1)} copy(bf16[12,24,96,32,4]{2,1,4,3,0:T(8,128)(2,1)} %broadcast_select_fusion) | data formatting | bytes 14155776 | tf_op jit(solution)/shard_map/jit(_take)/select_n | solution.py:38
  71.9 7.9 all-to-all-start
  81.8 206.9 %all-to-all-done = bf16[12,24,96,32,4]{2,1,4,0,3:T(8,128)(2,1)} async-done(((bf16[12,24,96,32,4]{2,1,4,0,3:T(8,128)(2,1)}), bf16[12,24,96,32,4]{2,1,4,0,3:T(8,128)(2,1)}, u32[]{:S(2)}, u32[]{:S(2)}) %all-to-all-start) | async-done | bytes 7077920 | tf_op jit(solution)/shard_map/all_to_all | solution.py:42
  288.7 10.2 %copy.48 = bf16[4,8,12,4,24,96]{5,4,3,2,1,0:T(8,128)(2,1)} copy(bf16[4,8,12,4,24,96]{5,4,0,2,3,1:T(8,128)(2,1)} %bitcast.9) | data formatting | bytes 14155776 | tf_op jit(solution)/shard_map/transpose | solution.py:45
  298.9 16.0 %pad_maximum_fusion = bf16[2,2,192,96,96]{4,3,2,1,0:T(8,128)(2,1)} fusion(bf16[2,2,96,96,96]{4,3,2,1,0:T(8,128)(2,1)} %bitcast.111), kind=kLoop, calls=%fused_computation.16 | loop fusion | flops 7077888 | bytes 21233664 | tf_op jit(solution)/shard_map/vmap(vmap(jit(_roll_dynamic)))/concatenate | solution.py:52
  314.9 5.1 broadcast.265.clone.1
  320.1 14.5 %while.6 = (s32[]{:T(128)}, bf16[2,2,192,96,96]{4,3,2,1,0:T(8,128)(2,1)}, s32[2,4]{1,0:T(2,128)S(1)}, bf16[2,2,96,96,96]{4,3,2,1,0:T(8,128)(2,1)}, s32[]{:T(128)}) while((s32[]{:T(128)}, bf16[2,2,192,96,96]{4,3,2,1,0:T(8,128)(2,1)}, s32[2,4]{1,0:T(2,128)S(1)}, bf16[2,2,96,96,96]{4,3,2,1,0:T(8,128)(2,1)}, s32[]{:T(128)}) %tuple.99), condition=%wide.while_cond, body=%wide.while_body.sunk | while | flops 2 | bytes 9438833 | solution.py:52
  320.7 6.7 dynamic-slice_dynamic-update-slice_fusion.10
  328.1 6.5 dynamic-slice_dynamic-update-slice_fusion.10
  334.6 18.2 %pad_maximum_fusion.1 = bf16[2,2,96,192,96]{4,3,2,1,0:T(8,128)(2,1)} fusion(bf16[2,2,96,96,96]{4,3,2,1,0:T(8,128)(2,1)} %get-tuple-element.12), kind=kLoop, calls=%fused_computation.17 | loop fusion | flops 28311552 | bytes 21233664 | tf_op jit(solution)/shard_map/vmap(vmap(jit(_roll_dynamic)))/concatenate | solution.py:53
  352.8 5.1 broadcast.265
  357.9 18.6 %while.7 = (s32[]{:T(128)}, bf16[2,2,96,192,96]{4,3,2,1,0:T(8,128)(2,1)}, s32[2,4]{1,0:T(2,128)S(1)}, bf16[2,2,96,96,96]{4,3,2,1,0:T(8,128)(2,1)}, s32[]{:T(128)}) while((s32[]{:T(128)}, bf16[2,2,96,192,96]{4,3,2,1,0:T(8,128)(2,1)}, s32[2,4]{1,0:T(2,128)S(1)}, bf16[2,2,96,96,96]{4,3,2,1,0:T(8,128)(2,1)}, s32[]{:T(128)}) %tuple.102), condition=%wide.while_cond.1, body=%wide.while_body.1.sunk | while | flops 2 | bytes 9438833 | solution.py:53
  358.6 8.7 %dynamic-slice_dynamic-update-slice_fusion.11 = bf16[2,2,96,96,96]{4,3,2,1,0:T(8,128)(2,1)} fusion(bf16[2,2,96,96,96]{4,3,2,1,0:T(8,128)(2,1)} %get-tuple-element.323, s32[]{:T(128)} %get-tuple-element.320, bf16[2,2,96,192,96]{4,3,2,1,0:T(8,128)(2,1)} %get-tuple-element.326, s32[]{:T(128)} %bitcast.98, s32[]{:T(128)} %bitcast.99), kind=kLoop, calls=%fused_computation.4.clone.1 | loop fusion | bytes 9438720 | tf_op jit(solution)/shard_map/vmap(vmap(jit(_roll_dynamic)))/gather
  368.0 8.6 %dynamic-slice_dynamic-update-slice_fusion.11 = bf16[2,2,96,96,96]{4,3,2,1,0:T(8,128)(2,1)} fusion(bf16[2,2,96,96,96]{4,3,2,1,0:T(8,128)(2,1)} %get-tuple-element.323, s32[]{:T(128)} %get-tuple-element.320, bf16[2,2,96,192,96]{4,3,2,1,0:T(8,128)(2,1)} %get-tuple-element.326, s32[]{:T(128)} %bitcast.98, s32[]{:T(128)} %bitcast.99), kind=kLoop, calls=%fused_computation.4.clone.1 | loop fusion | bytes 9438720 | tf_op jit(solution)/shard_map/vmap(vmap(jit(_roll_dynamic)))/gather
  376.5 20.0 %pad_maximum_fusion.2 = bf16[2,2,96,96,192]{4,3,2,1,0:T(8,128)(2,1)} fusion(bf16[2,2,96,96,96]{4,3,2,1,0:T(8,128)(2,1)} %get-tuple-element.20), kind=kLoop, calls=%fused_computation.18 | loop fusion | flops 28311552 | bytes 21233664 | tf_op jit(solution)/shard_map/vmap(vmap(jit(_roll_dynamic)))/concatenate | solution.py:54
  396.6 18.8 %while.8 = (s32[]{:T(128)}, bf16[2,2,96,96,192]{4,3,2,1,0:T(8,128)(2,1)}, s32[2,4]{1,0:T(2,128)S(1)}, bf16[2,2,96,96,96]{4,3,2,0,1:T(8,128)(2,1)}, s32[]{:T(128)}) while((s32[]{:T(128)}, bf16[2,2,96,96,192]{4,3,2,1,0:T(8,128)(2,1)}, s32[2,4]{1,0:T(2,128)S(1)}, bf16[2,2,96,96,96]{4,3,2,0,1:T(8,128)(2,1)}, s32[]{:T(128)}) %tuple.105), condition=%wide.while_cond.2, body=%wide.while_body.2.sunk | while | flops 2 | bytes 9438833 | solution.py:54
  397.2 8.7 %bitcast_dynamic-update-slice_fusion.2 = bf16[2,2,96,96,96]{4,3,2,0,1:T(8,128)(2,1)} fusion(bf16[2,2,96,96,96]{4,3,2,0,1:T(8,128)(2,1)} %get-tuple-element.338, s32[]{:T(128)} %get-tuple-element.335, bf16[2,2,96,96,192]{4,3,2,1,0:T(8,128)(2,1)} %get-tuple-element.341, s32[]{:T(128)} %bitcast.101, s32[]{:T(128)} %bitcast.102), kind=kLoop, calls=%fused_computation.6.clone.1 | loop fusion | bytes 9438720 | tf_op jit(solution)/shard_map/vmap(vmap(jit(_roll_dynamic)))/gather
  406.5 8.8 %bitcast_dynamic-update-slice_fusion.2 = bf16[2,2,96,96,96]{4,3,2,0,1:T(8,128)(2,1)} fusion(bf16[2,2,96,96,96]{4,3,2,0,1:T(8,128)(2,1)} %get-tuple-element.338, s32[]{:T(128)} %get-tuple-element.335, bf16[2,2,96,96,192]{4,3,2,1,0:T(8,128)(2,1)} %get-tuple-element.341, s32[]{:T(128)} %bitcast.101, s32[]{:T(128)} %bitcast.102), kind=kLoop, calls=%fused_computation.6.clone.1 | loop fusion | bytes 9438720 | tf_op jit(solution)/shard_map/vmap(vmap(jit(_roll_dynamic)))/gather
  418.6 6.4 fusion.17
  425.0 6.6 fusion.13
  431.7 3.8 fusion.23
  435.5 6.4 fusion.20
  441.9 6.8 fusion.9
  448.7 5.3 fusion.4
  454.8 4.5 pad_maximum_fusion.3
  462.1 10.2 %while.9 = (s32[]{:T(128)}, bf16[2,192,96,96]{3,2,1,0:T(8,128)(2,1)}, s32[2,4]{1,0:T(2,128)S(1)}, bf16[2,96,96,96]{3,2,1,0:T(8,128)(2,1)}, s32[]{:T(128)}) while((s32[]{:T(128)}, bf16[2,192,96,96]{3,2,1,0:T(8,128)(2,1)}, s32[2,4]{1,0:T(2,128)S(1)}, bf16[2,96,96,96]{3,2,1,0:T(8,128)(2,1)}, s32[]{:T(128)}) %tuple.108), condition=%wide.while_cond.3, body=%wide.while_body.3.sunk | while | flops 2 | bytes 4720241 | solution.py:70
  462.7 4.5 dynamic-slice_dynamic-update-slice_fusion.12
  467.8 4.5 dynamic-slice_dynamic-update-slice_fusion.12
  472.2 10.1 %pad_maximum_fusion.4 = bf16[2,96,192,96]{3,2,1,0:T(8,128)(2,1)} fusion(bf16[2,96,96,96]{3,2,1,0:T(8,128)(2,1)} %get-tuple-element.36), kind=kLoop, calls=%fused_computation.22 | loop fusion | flops 14155776 | bytes 10616832 | tf_op jit(solution)/shard_map/vmap(jit(_roll_dynamic))/concatenate | solution.py:71
  485.0 12.3 %while.10 = (s32[]{:T(128)}, bf16[2,96,192,96]{3,2,1,0:T(8,128)(2,1)}, s32[2,4]{1,0:T(2,128)S(1)}, bf16[2,96,96,96]{3,2,1,0:T(8,128)(2,1)}, s32[]{:T(128)}) while((s32[]{:T(128)}, bf16[2,96,192,96]{3,2,1,0:T(8,128)(2,1)}, s32[2,4]{1,0:T(2,128)S(1)}, bf16[2,96,96,96]{3,2,1,0:T(8,128)(2,1)}, s32[]{:T(128)}) %tuple.111), condition=%wide.while_cond.4, body=%wide.while_body.4.sunk | while | flops 2 | bytes 4720241 | solution.py:71
  485.7 5.5 dynamic-slice_dynamic-update-slice_fusion.13
  491.8 5.5 dynamic-slice_dynamic-update-slice_fusion.13
  497.4 11.6 %pad_maximum_fusion.5 = bf16[2,96,96,192]{3,2,1,0:T(8,128)(2,1)} fusion(bf16[2,96,96,96]{3,2,1,0:T(8,128)(2,1)} %get-tuple-element.44), kind=kLoop, calls=%fused_computation.23 | loop fusion | flops 14155776 | bytes 10616832 | tf_op jit(solution)/shard_map/vmap(jit(_roll_dynamic))/concatenate | solution.py:72
  511.7 12.9 %while.11 = (s32[]{:T(128)}, bf16[2,96,96,192]{3,2,1,0:T(8,128)(2,1)}, s32[2,4]{1,0:T(2,128)S(1)}, bf16[2,96,96,96]{3,2,1,0:T(8,128)(2,1)}, s32[]{:T(128)}) while((s32[]{:T(128)}, bf16[2,96,96,192]{3,2,1,0:T(8,128)(2,1)}, s32[2,4]{1,0:T(2,128)S(1)}, bf16[2,96,96,96]{3,2,1,0:T(8,128)(2,1)}, s32[]{:T(128)}) %tuple.114), condition=%wide.while_cond.5, body=%wide.while_body.5.sunk | while | flops 2 | bytes 4720241 | solution.py:72
  512.3 5.8 dynamic-slice_dynamic-update-slice_fusion.14
  518.8 5.8 dynamic-slice_dynamic-update-slice_fusion.14
  524.6 3.7 copy.61
  535.5 105.1 %all-to-all-done.1 = bf16[12,24,96,32,2]{2,1,4,0,3:T(8,128)(2,1)} async-done(((bf16[12,24,96,32,2]{2,1,4,0,3:T(8,128)(2,1)}), bf16[12,24,96,32,2]{2,1,4,0,3:T(8,128)(2,1)}, u32[]{:S(2)}, u32[]{:S(2)}) %all-to-all-start.1) | async-done | bytes 3538976 | tf_op jit(solution)/shard_map/all_to_all | solution.py:80
  640.6 5.3 copy.63
  646.0 8.1 reshape_reshape.4
  654.1 12.0 %fusion.32 = f32[27648,256]{1,0:T(8,128)} fusion(bf16[27648,64]{0,1:T(8,128)(2,1)S(1)} %reshape_reshape.4, s32[64]{0:T(128)S(1)} %slice_bitcast_fusion), kind=kOutput, calls=%fused_computation.49 | convolution fusion | flops 905986048 | bytes 31850752 | tf_op jit(solution)/shard_map/dot_general | solution.py:83
  666.1 17.6 %fusion.28 = f32[256,256]{0,1:T(8,128)} fusion(bf16[27648,256]{1,0:T(8,128)(2,1)} %bitcast.109, f32[27648,256]{1,0:T(8,128)} %fusion.32), kind=kOutput, calls=%fused_computation.44 | convolution fusion | flops 3630956544 | bytes 42729472 | tf_op jit(solution)/shard_map/dot_general | solution.py:86
  683.8 126.0 %all-reduce.7.cloned.1.call-done = f32[256,256]{0,1:T(8,128)} async-done(((f32[256,256]{0,1:T(8,128)}), f32[256,256]{0,1:T(8,128)}) %all-reduce.7.cloned.1.call-update) | async-done | bytes 262160 | tf_op jit(solution)/shard_map/psum | solution.py:89
  809.7 25.2 %fusion = f32[27648,256]{1,0:T(8,128)} fusion(f32[27648,256]{1,0:T(8,128)} %fusion.32, bf16[27648,256]{1,0:T(8,128)(2,1)} %bitcast.110, f32[256,256]{0,1:T(8,128)} %all-reduce.7.cloned.1.call-done), kind=kOutput, calls=%fused_computation.15 | convolution fusion | flops 3631087616 | bytes 71041024 | tf_op jit(solution)/shard_map/dot_general | solution.py:91
  (63 shorter events, 29.7 us)
Async XLA Ops:
  71.9 7.9 copy-start
  71.9 8.9 %copy-start.2 = (s32[64]{0:T(128)S(1)}, s32[64]{0:T(128)}, u32[]{:S(2)}) copy-start(s32[64]{0:T(128)} %param.7) | copy-start | bytes 772
  71.9 216.8 %all-to-all-start = ((bf16[12,24,96,32,4]{2,1,4,0,3:T(8,128)(2,1)}), bf16[12,24,96,32,4]{2,1,4,0,3:T(8,128)(2,1)}, u32[]{:S(2)}, u32[]{:S(2)}) async-start(bf16[12,24,96,32,4]{2,1,4,0,3:T(8,128)(2,1)} %copy.46), calls=%async_computation | async-start | bytes 18874368 | tf_op jit(solution)/shard_map/all_to_all | solution.py:42
  528.3 7.2 copy-start.1
  531.9 108.8 %all-to-all-start.1 = ((bf16[12,24,96,32,2]{2,1,4,0,3:T(8,128)(2,1)}), bf16[12,24,96,32,2]{2,1,4,0,3:T(8,128)(2,1)}, u32[]{:S(2)}, u32[]{:S(2)}) async-start(bf16[12,24,96,32,2]{2,1,4,0,3:T(8,128)(2,1)} %copy.62), calls=%async_computation.1 | async-start | bytes 9437184 | tf_op jit(solution)/shard_map/all_to_all | solution.py:80
  535.5 274.3 %all-reduce.7.cloned.1.call-start = ((), (), s32[]{:S(2)}) async-start(), calls=%async_computation.2 | async-start | bytes 524288 | tf_op jit(solution)/shard_map/psum | solution.py:89
Sparse Core Ops, SparseCore 0:
  683.9 125.7 all-reduce.6
where the time goes:
time: 849 us; the launch traced here: 842 us
  waiting for transfers between devices  438 us (52%)
  local copies, waits for them, and re-layouts  195 us (23%)
  other arithmetic  93.4 us (11%)
  matrix products  90.2 us (11%)
  between operations  13.9 us (2%)
  starting transfers between devices  11.5 us (1%)
    all_to_all x1, waiting for transfers between devices, body(): lax.all_to_all(flat_send, ('gz', 'gy'), split_axis=3, concat_axis=3, tile...  207 us
    psum x1, waiting for transfers between devices, body(): summed = lax.psum(partial_tiles, ('gz', 'gy'))  126 us
    all_to_all x1, waiting for transfers between devices, body(): lax.all_to_all(flat_back, ('gz', 'gy'), split_axis=3, concat_axis=3, tile...  105 us
    gather x36, local copies, waits for them, and re-layouts  87.1 us
    unnamed x15, local copies, waits for them, and re-layouts  41.7 us
    dot_general x1, matrix products, body(): gradient = action - jnp.dot(flat, tiles, preferred_element_type=jnp.float32)  25.2 us
    gather x2, local copies, waits for them, and re-layouts, body(): chosen = jnp.take(orbitals, pair_list.reshape(-1), axis=3)  23.2 us
    concatenate x1, other arithmetic, cut_box(): grid = jnp.roll(grid, -anchor[2], axis=2)  20 us
  transfers between devices with their start and end apart: 3, of which 3 were waited for; matrix products, arithmetic and copies ran while one was open for 0% of the time, Pallas kernels for 0%

commit v1 on v0

--- a/solution.py
+++ b/solution.py
@@ -86,7 +86,7 @@
     partial_tiles = lax.dot_general(
         flat, action_low, (((0,), (0,)), ((), ())), preferred_element_type=jnp.float32
     )
-    summed = lax.psum(partial_tiles, ("gz", "gy"))
+    summed = lax.psum(lax.psum(partial_tiles, "gy"), "gz")
     tiles = (summed / (float(B) ** 3 / 4.0)).astype(jnp.bfloat16)
     gradient = action - jnp.dot(flat, tiles, preferred_element_type=jnp.float32)
     return gradient.reshape(depth, rows, across, norb)

time: 849 us -> 830 us (0.978)
  waiting for transfers between devices: 438 us -> 418 us
    psum x1 -> x2, waiting for transfers between devices: 126 us -> 106 us  [body(): summed = lax.psum(lax.psum(partial_tiles, 'gy'), 'gz')]
  transfers between devices with their start and end apart: 3 -> 4, of which waited for: 3 -> 4; matrix products, arithmetic and copies ran while one was open for 0% -> 0% of each run, Pallas kernels for 0% -> 0%
where the time goes in v1:
time: 830 us; the launch traced here: 822 us
  waiting for transfers between devices  418 us (50%)
  local copies, waits for them, and re-layouts  195 us (23%)
  other arithmetic  93.4 us (11%)
  matrix products  90.3 us (11%)
  between operations  13.9 us (2%)
  starting transfers between devices  11.6 us (1%)
    all_to_all x1, waiting for transfers between devices, body(): lax.all_to_all(flat_send, ('gz', 'gy'), split_axis=3, concat_axis=3, tile...  207 us
    psum x2, waiting for transfers between devices, body(): summed = lax.psum(lax.psum(partial_tiles, 'gy'), 'gz')  106 us
    all_to_all x1, waiting for transfers between devices, body(): lax.all_to_all(flat_back, ('gz', 'gy'), split_axis=3, concat_axis=3, tile...  105 us
    gather x36, local copies, waits for them, and re-layouts  87.1 us
    unnamed x15, local copies, waits for them, and re-layouts  41.7 us
    dot_general x1, matrix products, body(): gradient = action - jnp.dot(flat, tiles, preferred_element_type=jnp.float32)  25.2 us
    gather x2, local copies, waits for them, and re-layouts, body(): chosen = jnp.take(orbitals, pair_list.reshape(-1), axis=3)  23.2 us
    concatenate x1, other arithmetic, cut_box(): grid = jnp.roll(grid, -anchor[2], axis=2)  20 us
  transfers between devices with their start and end apart: 4, of which 4 were waited for; matrix products, arithmetic and copies ran while one was open for 0% of the time, Pallas kernels for 0%

profile of v1, /device:TPU:0, one launch (start us, length us, event | category | flops | bytes accessed | tf_op | source)
XLA Modules:
  0.0 822.1 jit_solution(18044069387482050391)
XLA Ops:
  7.5 22.4 %copy.44 = bf16[12,24,96,256]{2,1,0,3:T(8,128)(2,1)} copy(bf16[12,24,96,256]{3,2,1,0:T(8,128)(2,1)} %param.4) | data formatting | bytes 28311552 | tf_op args[0]
  29.9 13.6 %gather_fusion = bf16[128,12,24,96]{3,2,1,0:T(8,128)(2,1)} fusion(bf16[12,24,96,256]{2,1,0,3:T(8,128)(2,1)} %copy.44, s32[1024]{0:T(1024)S(1)} %pad_clamp_fusion.1), kind=kCustom, calls=%fused_computation | custom fusion | bytes 14156288 | tf_op jit(solution)/shard_map/jit(_take)/gather | solution.py:38
  43.5 9.6 %copy.45 = bf16[12,24,96,128]{2,1,3,0:T(8,128)(2,1)} copy(bf16[12,24,96,128]{2,1,0,3:T(8,128)(2,1)} %bitcast.113) | data formatting | bytes 14155776 | tf_op jit(solution)/shard_map/jit(_take)/gather | solution.py:38
  53.2 8.6 %broadcast_select_fusion = bf16[12,24,96,32,4]{2,1,4,3,0:T(8,128)(2,1)} fusion(bf16[12,24,96,32,4]{2,1,4,3,0:T(8,128)(2,1)} %bitcast.112, pred[32,4]{1,0:T(8,128)(4,1)S(1)} %compare_and_fusion), kind=kLoop, calls=%fused_computation.24 | loop fusion | flops 3538944 | bytes 14155904 | tf_op jit(solution)/shard_map/jit(_take)/select_n | solution.py:38
  61.7 10.2 %copy.46 = bf16[12,24,96,32,4]{2,1,4,0,3:T(8,128)(2,1)} copy(bf16[12,24,96,32,4]{2,1,4,3,0:T(8,128)(2,1)} %broadcast_select_fusion) | data formatting | bytes 14155776 | tf_op jit(solution)/shard_map/jit(_take)/select_n | solution.py:38
  71.9 7.9 all-to-all-start
  81.8 206.9 %all-to-all-done = bf16[12,24,96,32,4]{2,1,4,0,3:T(8,128)(2,1)} async-done(((bf16[12,24,96,32,4]{2,1,4,0,3:T(8,128)(2,1)}), bf16[12,24,96,32,4]{2,1,4,0,3:T(8,128)(2,1)}, u32[]{:S(2)}, u32[]{:S(2)}) %all-to-all-start) | async-done | bytes 7077920 | tf_op jit(solution)/shard_map/all_to_all | solution.py:42
  288.7 10.2 %copy.48 = bf16[4,8,12,4,24,96]{5,4,3,2,1,0:T(8,128)(2,1)} copy(bf16[4,8,12,4,24,96]{5,4,0,2,3,1:T(8,128)(2,1)} %bitcast.9) | data formatting | bytes 14155776 | tf_op jit(solution)/shard_map/transpose | solution.py:45
  298.9 16.0 %pad_maximum_fusion = bf16[2,2,192,96,96]{4,3,2,1,0:T(8,128)(2,1)} fusion(bf16[2,2,96,96,96]{4,3,2,1,0:T(8,128)(2,1)} %bitcast.111), kind=kLoop, calls=%fused_computation.16 | loop fusion | flops 7077888 | bytes 21233664 | tf_op jit(solution)/shard_map/vmap(vmap(jit(_roll_dynamic)))/concatenate | solution.py:52
  314.9 5.1 broadcast.265.clone.1
  320.1 14.5 %while.6 = (s32[]{:T(128)}, bf16[2,2,192,96,96]{4,3,2,1,0:T(8,128)(2,1)}, s32[2,4]{1,0:T(2,128)S(1)}, bf16[2,2,96,96,96]{4,3,2,1,0:T(8,128)(2,1)}, s32[]{:T(128)}) while((s32[]{:T(128)}, bf16[2,2,192,96,96]{4,3,2,1,0:T(8,128)(2,1)}, s32[2,4]{1,0:T(2,128)S(1)}, bf16[2,2,96,96,96]{4,3,2,1,0:T(8,128)(2,1)}, s32[]{:T(128)}) %tuple.99), condition=%wide.while_cond, body=%wide.while_body.sunk | while | flops 2 | bytes 9438833 | solution.py:52
  320.7 6.7 dynamic-slice_dynamic-update-slice_fusion.10
  328.1 6.5 dynamic-slice_dynamic-update-slice_fusion.10
  334.6 18.2 %pad_maximum_fusion.1 = bf16[2,2,96,192,96]{4,3,2,1,0:T(8,128)(2,1)} fusion(bf16[2,2,96,96,96]{4,3,2,1,0:T(8,128)(2,1)} %get-tuple-element.12), kind=kLoop, calls=%fused_computation.17 | loop fusion | flops 28311552 | bytes 21233664 | tf_op jit(solution)/shard_map/vmap(vmap(jit(_roll_dynamic)))/concatenate | solution.py:53
  352.8 5.1 broadcast.265
  357.9 18.6 %while.7 = (s32[]{:T(128)}, bf16[2,2,96,192,96]{4,3,2,1,0:T(8,128)(2,1)}, s32[2,4]{1,0:T(2,128)S(1)}, bf16[2,2,96,96,96]{4,3,2,1,0:T(8,128)(2,1)}, s32[]{:T(128)}) while((s32[]{:T(128)}, bf16[2,2,96,192,96]{4,3,2,1,0:T(8,128)(2,1)}, s32[2,4]{1,0:T(2,128)S(1)}, bf16[2,2,96,96,96]{4,3,2,1,0:T(8,128)(2,1)}, s32[]{:T(128)}) %tuple.102), condition=%wide.while_cond.1, body=%wide.while_body.1.sunk | while | flops 2 | bytes 9438833 | solution.py:53
  358.6 8.7 %dynamic-slice_dynamic-update-slice_fusion.11 = bf16[2,2,96,96,96]{4,3,2,1,0:T(8,128)(2,1)} fusion(bf16[2,2,96,96,96]{4,3,2,1,0:T(8,128)(2,1)} %get-tuple-element.323, s32[]{:T(128)} %get-tuple-element.320, bf16[2,2,96,192,96]{4,3,2,1,0:T(8,128)(2,1)} %get-tuple-element.326, s32[]{:T(128)} %bitcast.98, s32[]{:T(128)} %bitcast.99), kind=kLoop, calls=%fused_computation.4.clone.1 | loop fusion | bytes 9438720 | tf_op jit(solution)/shard_map/vmap(vmap(jit(_roll_dynamic)))/gather
  368.0 8.6 %dynamic-slice_dynamic-update-slice_fusion.11 = bf16[2,2,96,96,96]{4,3,2,1,0:T(8,128)(2,1)} fusion(bf16[2,2,96,96,96]{4,3,2,1,0:T(8,128)(2,1)} %get-tuple-element.323, s32[]{:T(128)} %get-tuple-element.320, bf16[2,2,96,192,96]{4,3,2,1,0:T(8,128)(2,1)} %get-tuple-element.326, s32[]{:T(128)} %bitcast.98, s32[]{:T(128)} %bitcast.99), kind=kLoop, calls=%fused_computation.4.clone.1 | loop fusion | bytes 9438720 | tf_op jit(solution)/shard_map/vmap(vmap(jit(_roll_dynamic)))/gather
  376.5 20.0 %pad_maximum_fusion.2 = bf16[2,2,96,96,192]{4,3,2,1,0:T(8,128)(2,1)} fusion(bf16[2,2,96,96,96]{4,3,2,1,0:T(8,128)(2,1)} %get-tuple-element.20), kind=kLoop, calls=%fused_computation.18 | loop fusion | flops 28311552 | bytes 21233664 | tf_op jit(solution)/shard_map/vmap(vmap(jit(_roll_dynamic)))/concatenate | solution.py:54
  396.6 18.8 %while.8 = (s32[]{:T(128)}, bf16[2,2,96,96,192]{4,3,2,1,0:T(8,128)(2,1)}, s32[2,4]{1,0:T(2,128)S(1)}, bf16[2,2,96,96,96]{4,3,2,0,1:T(8,128)(2,1)}, s32[]{:T(128)}) while((s32[]{:T(128)}, bf16[2,2,96,96,192]{4,3,2,1,0:T(8,128)(2,1)}, s32[2,4]{1,0:T(2,128)S(1)}, bf16[2,2,96,96,96]{4,3,2,0,1:T(8,128)(2,1)}, s32[]{:T(128)}) %tuple.105), condition=%wide.while_cond.2, body=%wide.while_body.2.sunk | while | flops 2 | bytes 9438833 | solution.py:54
  397.2 8.7 %bitcast_dynamic-update-slice_fusion.2 = bf16[2,2,96,96,96]{4,3,2,0,1:T(8,128)(2,1)} fusion(bf16[2,2,96,96,96]{4,3,2,0,1:T(8,128)(2,1)} %get-tuple-element.338, s32[]{:T(128)} %get-tuple-element.335, bf16[2,2,96,96,192]{4,3,2,1,0:T(8,128)(2,1)} %get-tuple-element.341, s32[]{:T(128)} %bitcast.101, s32[]{:T(128)} %bitcast.102), kind=kLoop, calls=%fused_computation.6.clone.1 | loop fusion | bytes 9438720 | tf_op jit(solution)/shard_map/vmap(vmap(jit(_roll_dynamic)))/gather
  406.5 8.8 %bitcast_dynamic-update-slice_fusion.2 = bf16[2,2,96,96,96]{4,3,2,0,1:T(8,128)(2,1)} fusion(bf16[2,2,96,96,96]{4,3,2,0,1:T(8,128)(2,1)} %get-tuple-element.338, s32[]{:T(128)} %get-tuple-element.335, bf16[2,2,96,96,192]{4,3,2,1,0:T(8,128)(2,1)} %get-tuple-element.341, s32[]{:T(128)} %bitcast.101, s32[]{:T(128)} %bitcast.102), kind=kLoop, calls=%fused_computation.6.clone.1 | loop fusion | bytes 9438720 | tf_op jit(solution)/shard_map/vmap(vmap(jit(_roll_dynamic)))/gather
  418.6 6.4 fusion.17
  425.0 6.6 fusion.13
  431.7 3.8 fusion.23
  435.5 6.4 fusion.20
  441.9 6.8 fusion.9
  448.7 5.3 fusion.4
  454.8 4.5 pad_maximum_fusion.3
  462.1 10.2 %while.9 = (s32[]{:T(128)}, bf16[2,192,96,96]{3,2,1,0:T(8,128)(2,1)}, s32[2,4]{1,0:T(2,128)S(1)}, bf16[2,96,96,96]{3,2,1,0:T(8,128)(2,1)}, s32[]{:T(128)}) while((s32[]{:T(128)}, bf16[2,192,96,96]{3,2,1,0:T(8,128)(2,1)}, s32[2,4]{1,0:T(2,128)S(1)}, bf16[2,96,96,96]{3,2,1,0:T(8,128)(2,1)}, s32[]{:T(128)}) %tuple.108), condition=%wide.while_cond.3, body=%wide.while_body.3.sunk | while | flops 2 | bytes 4720241 | solution.py:70
  462.7 4.5 dynamic-slice_dynamic-update-slice_fusion.12
  467.8 4.5 dynamic-slice_dynamic-update-slice_fusion.12
  472.2 10.1 %pad_maximum_fusion.4 = bf16[2,96,192,96]{3,2,1,0:T(8,128)(2,1)} fusion(bf16[2,96,96,96]{3,2,1,0:T(8,128)(2,1)} %get-tuple-element.36), kind=kLoop, calls=%fused_computation.22 | loop fusion | flops 14155776 | bytes 10616832 | tf_op jit(solution)/shard_map/vmap(jit(_roll_dynamic))/concatenate | solution.py:71
  485.0 12.3 %while.10 = (s32[]{:T(128)}, bf16[2,96,192,96]{3,2,1,0:T(8,128)(2,1)}, s32[2,4]{1,0:T(2,128)S(1)}, bf16[2,96,96,96]{3,2,1,0:T(8,128)(2,1)}, s32[]{:T(128)}) while((s32[]{:T(128)}, bf16[2,96,192,96]{3,2,1,0:T(8,128)(2,1)}, s32[2,4]{1,0:T(2,128)S(1)}, bf16[2,96,96,96]{3,2,1,0:T(8,128)(2,1)}, s32[]{:T(128)}) %tuple.111), condition=%wide.while_cond.4, body=%wide.while_body.4.sunk | while | flops 2 | bytes 4720241 | solution.py:71
  485.7 5.5 dynamic-slice_dynamic-update-slice_fusion.13
  491.8 5.5 dynamic-slice_dynamic-update-slice_fusion.13
  497.4 11.6 %pad_maximum_fusion.5 = bf16[2,96,96,192]{3,2,1,0:T(8,128)(2,1)} fusion(bf16[2,96,96,96]{3,2,1,0:T(8,128)(2,1)} %get-tuple-element.44), kind=kLoop, calls=%fused_computation.23 | loop fusion | flops 14155776 | bytes 10616832 | tf_op jit(solution)/shard_map/vmap(jit(_roll_dynamic))/concatenate | solution.py:72
  511.7 12.9 %while.11 = (s32[]{:T(128)}, bf16[2,96,96,192]{3,2,1,0:T(8,128)(2,1)}, s32[2,4]{1,0:T(2,128)S(1)}, bf16[2,96,96,96]{3,2,1,0:T(8,128)(2,1)}, s32[]{:T(128)}) while((s32[]{:T(128)}, bf16[2,96,96,192]{3,2,1,0:T(8,128)(2,1)}, s32[2,4]{1,0:T(2,128)S(1)}, bf16[2,96,96,96]{3,2,1,0:T(8,128)(2,1)}, s32[]{:T(128)}) %tuple.114), condition=%wide.while_cond.5, body=%wide.while_body.5.sunk | while | flops 2 | bytes 4720241 | solution.py:72
  512.3 5.8 dynamic-slice_dynamic-update-slice_fusion.14
  518.8 5.8 dynamic-slice_dynamic-update-slice_fusion.14
  535.5 105.1 %all-to-all-done.1 = bf16[12,24,96,32,2]{2,1,4,0,3:T(8,128)(2,1)} async-done(((bf16[12,24,96,32,2]{2,1,4,0,3:T(8,128)(2,1)}), bf16[12,24,96,32,2]{2,1,4,0,3:T(8,128)(2,1)}, u32[]{:S(2)}, u32[]{:S(2)}) %all-to-all-start.1) | async-done | bytes 3538976 | tf_op jit(solution)/shard_map/all_to_all | solution.py:80
  640.6 5.3 copy.63
  646.0 8.1 reshape_reshape.4
  654.1 12.0 %fusion.32 = f32[27648,256]{1,0:T(8,128)} fusion(bf16[27648,64]{0,1:T(8,128)(2,1)S(1)} %reshape_reshape.4, s32[64]{0:T(128)S(1)} %slice_bitcast_fusion), kind=kOutput, calls=%fused_computation.49 | convolution fusion | flops 905986048 | bytes 31850752 | tf_op jit(solution)/shard_map/dot_general | solution.py:83
  666.1 17.6 %fusion.28 = f32[256,256]{0,1:T(8,128)} fusion(bf16[27648,256]{1,0:T(8,128)(2,1)} %bitcast.109, f32[27648,256]{1,0:T(8,128)} %fusion.32), kind=kOutput, calls=%fused_computation.44 | convolution fusion | flops 3630956544 | bytes 42729472 | tf_op jit(solution)/shard_map/dot_general | solution.py:86
  683.8 31.6 %all-reduce.8.cloned.1.call-done = f32[256,256]{0,1:T(8,128)} async-done(((f32[256,256]{0,1:T(8,128)}), f32[256,256]{0,1:T(8,128)}) %all-reduce.8.cloned.1.call-update) | async-done | bytes 262160 | tf_op jit(solution)/shard_map/psum | solution.py:89
  715.5 74.4 %all-reduce.10.cloned.1.call-done = f32[256,256]{0,1:T(8,128)} async-done(((f32[256,256]{0,1:T(8,128)}), f32[256,256]{0,1:T(8,128)}) %all-reduce.10.cloned.1.call-update) | async-done | bytes 262160 | tf_op jit(solution)/shard_map/psum | solution.py:89
  789.8 25.2 %fusion = f32[27648,256]{1,0:T(8,128)} fusion(f32[27648,256]{1,0:T(8,128)} %fusion.32, bf16[27648,256]{1,0:T(8,128)(2,1)} %bitcast.110, f32[256,256]{0,1:T(8,128)} %all-reduce.10.cloned.1.call-done), kind=kOutput, calls=%fused_computation.15 | convolution fusion | flops 3631087616 | bytes 71041024 | tf_op jit(solution)/shard_map/dot_general | solution.py:91
  (66 shorter events, 33.5 us)
Async XLA Ops:
  71.9 7.9 copy-start
  71.9 8.9 %copy-start.2 = (s32[64]{0:T(128)S(1)}, s32[64]{0:T(128)}, u32[]{:S(2)}) copy-start(s32[64]{0:T(128)} %param.7) | copy-start | bytes 772
  71.9 216.8 %all-to-all-start = ((bf16[12,24,96,32,4]{2,1,4,0,3:T(8,128)(2,1)}), bf16[12,24,96,32,4]{2,1,4,0,3:T(8,128)(2,1)}, u32[]{:S(2)}, u32[]{:S(2)}) async-start(bf16[12,24,96,32,4]{2,1,4,0,3:T(8,128)(2,1)} %copy.46), calls=%async_computation | async-start | bytes 18874368 | tf_op jit(solution)/shard_map/all_to_all | solution.py:42
  528.3 7.2 copy-start.1
  531.9 108.8 %all-to-all-start.1 = ((bf16[12,24,96,32,2]{2,1,4,0,3:T(8,128)(2,1)}), bf16[12,24,96,32,2]{2,1,4,0,3:T(8,128)(2,1)}, u32[]{:S(2)}, u32[]{:S(2)}) async-start(bf16[12,24,96,32,2]{2,1,4,0,3:T(8,128)(2,1)} %copy.62), calls=%async_computation.1 | async-start | bytes 9437184 | tf_op jit(solution)/shard_map/all_to_all | solution.py:80
  535.5 180.0 %all-reduce.8.cloned.1.call-start = ((), (), s32[]{:S(2)}) async-start(), calls=%async_computation.2 | async-start | bytes 524288 | tf_op jit(solution)/shard_map/psum | solution.py:89
  683.8 106.1 %all-reduce.10.cloned.1.call-start = ((), (), s32[]{:S(2)}) async-start(), calls=%async_computation.3 | async-start | bytes 524288 | tf_op jit(solution)/shard_map/psum | solution.py:89
Sparse Core Ops, SparseCore 0:
  683.9 31.4 all-reduce.7
  718.8 71.0 all-reduce.9
